TPU v7x, 1024 devices: a whole 4x4x32 slice. The times are simulated.
1024 devices in a mesh: aa: 16 (over y, x_hi, core), ba: 64 (over x_lo, z).
Axes of the slice: x: 4 (x_hi: 2, x_lo: 2; x = x_hi * 2 + x_lo), y: 4, z: 32, core: 2. Of those that a mesh axis runs over, the one named last changes fastest.
Arguments:
- state: float32 [14, 64, 64, 128], P(None, 'ba', 'aa'), as said below
- labels: int32 [64, 64, 128], P('ba', 'aa'), may hold values from 0 to 2, as said below
Outputs:
- swept: float32 [14, 64, 64, 128], P(None, 'ba', 'aa')
Inputs may be any that keep to these rules, and one draw needn't show every extreme that they name: `labels`: void cells lie in a band of low y and in scattered pores; projectile cells form one box inside the band. `state`: density is positive; inverse deformation gradients lie within 0.6 of the identity in every entry.
All inputs are finite; a program needn't handle non-finite values.
Results may differ from a plain program's by a relative error of at most 0.0003.
Values sent between devices are 32-bit elements; how exact they have to be, the bound alone decides.
A program may use at most 32 MiB of HBM per device.

v0:
```python
import functools

import jax
import jax.numpy as jnp
from jax import lax
from jax.sharding import Mesh
from jax.sharding import PartitionSpec as P

RETURN_ITERS = 2
BA = ("ba_0", "ba_1")
AA_BA = ("aa_0", "aa_1", "aa_2", "ba_0", "ba_1")
AA = ("aa_0", "aa_1", "aa_2")


GAMMA_TABLE = (3.0, 4.0, 1.4)
STIFF_TABLE = (1.0, 6.0, 0.0)
SHEAR_TABLE = (0.6, 3.0, 0.0)
COHESION_TABLE = (0.05, 0.0, 0.0)
FRICTION_TABLE = (0.4, 0.0, 0.0)
DENSITY_FLOOR = 0.2
TRACTION_FLOOR = 0.1
COURANT = 0.4
WENO_EPSILON = 1e-06


def in_blocks(value, dim, size):
    lengths = value.shape
    pieces = value.reshape(*lengths[:dim], size, lengths[dim] // size, *lengths[dim + 1 :])
    return jnp.moveaxis(pieces, dim, 0)


def joined_along(pieces, dim):
    lengths = list(pieces.shape[1:])
    lengths[dim] *= pieces.shape[0]
    return jnp.moveaxis(pieces, 0, dim).reshape(lengths)


def exchange_in_order(pieces, axes, turns):
    lengths = [lax.axis_size(a) for a in axes]
    pieces = pieces.reshape(*lengths, *pieces.shape[1:])
    for k in turns:
        pieces = lax.all_to_all(pieces, axes[k], split_axis=k, concat_axis=k, tiled=True)
    return pieces.reshape(-1, *pieces.shape[len(axes) :])


def exchange_by_axis(value, axes, turns, split_dim, concat_dim):
    pieces = in_blocks(value, split_dim, lax.axis_size(axes))
    return joined_along(exchange_in_order(pieces, axes, turns), concat_dim)


def over_axes(value, axes):
    return functools.reduce(lax.pmax, axes, value)


def padded_2(block, sides, width):
    for axis, dim in sides:
        count = lax.axis_size(axis)
        forward = [(i, i + 1) for i in range(count - 1)]
        backward = [(target, source) for source, target in forward]
        low = lax.ppermute(
            lax.slice_in_dim(block, block.shape[dim] - width, None, axis=dim), axis, forward
        )
        high = lax.ppermute(lax.slice_in_dim(block, 0, width, axis=dim), axis, backward)
        block = jnp.concatenate([low, block, high], axis=dim)
    return block


def material(label):

    def pick(table):
        return jnp.where(label == 0, table[0], jnp.where(label == 1, table[1], table[2]))

    return (
        pick(GAMMA_TABLE),
        pick(STIFF_TABLE),
        pick(SHEAR_TABLE),
        pick(COHESION_TABLE),
        pick(FRICTION_TABLE),
    )


def deviator(gradient, shear):
    metric = [
        [
            sum((gradient[row][first] * gradient[row][second] for row in range(3)))
            for second in range(3)
        ]
        for first in range(3)
    ]
    third = (metric[0][0] + metric[1][1] + metric[2][2]) / 3.0
    devs = [
        [metric[first][second] - (third if first == second else 0.0) for second in range(3)]
        for first in range(3)
    ]
    stress = [[-shear * devs[first][second] for second in range(3)] for first in range(3)]
    energy = (
        0.25
        * shear
        * sum(
            (devs[first][second] * devs[first][second] for first in range(3) for second in range(3))
        )
    )
    return (stress, energy)


def primitives(fields, label):
    gamma, stiff, shear, cohesion, friction = material(label)
    density = jnp.maximum(fields[0], DENSITY_FLOOR)
    velocity = [fields[1 + comp] / density for comp in range(3)]
    gradient = [[fields[5 + 3 * row + col] for col in range(3)] for row in range(3)]
    stress, energy = deviator(gradient, shear)
    kinetic = 0.5 * (fields[1] * velocity[0] + fields[2] * velocity[1] + fields[3] * velocity[2])
    pressure = (gamma - 1.0) * (fields[4] - kinetic - energy) - gamma * stiff
    sound = jnp.sqrt(
        (gamma * jnp.maximum(pressure + stiff, TRACTION_FLOOR) + 4.0 / 3.0 * shear) / density
    )
    return (density, velocity, gradient, stress, pressure, sound)


def weno_face(first, second, centre, fourth, fifth):
    cand_a = (2.0 * first - 7.0 * second + 11.0 * centre) / 6.0
    cand_b = (-second + 5.0 * centre + 2.0 * fourth) / 6.0
    cand_c = (2.0 * centre + 5.0 * fourth - fifth) / 6.0
    rough_a = (
        13.0 / 12.0 * (first - 2.0 * second + centre) ** 2
        + 0.25 * (first - 4.0 * second + 3.0 * centre) ** 2
    )
    rough_b = 13.0 / 12.0 * (second - 2.0 * centre + fourth) ** 2 + 0.25 * (second - fourth) ** 2
    rough_c = (
        13.0 / 12.0 * (centre - 2.0 * fourth + fifth) ** 2
        + 0.25 * (3.0 * centre - 4.0 * fourth + fifth) ** 2
    )
    weight_a = 0.1 / (WENO_EPSILON + rough_a) ** 2
    weight_b = 0.6 / (WENO_EPSILON + rough_b) ** 2
    weight_c = 0.3 / (WENO_EPSILON + rough_c) ** 2
    return (weight_a * cand_a + weight_b * cand_b + weight_c * cand_c) / (
        weight_a + weight_b + weight_c
    )


def riemann(left_fields, right_fields, left_label, right_label, direction):
    left = primitives(left_fields, left_label)
    right = primitives(right_fields, right_label)
    left_speed = left[1][direction]
    right_speed = right[1][direction]
    slow = jnp.minimum(left_speed - left[5], right_speed - right[5])
    fast = jnp.maximum(left_speed + left[5], right_speed + right[5])
    left_traction = left[4] - left[3][direction][direction]
    right_traction = right[4] - right[3][direction][direction]
    left_gap = slow - left_speed
    right_gap = fast - right_speed
    contact = (
        right_traction
        - left_traction
        + left[0] * left_speed * left_gap
        - right[0] * right_speed * right_gap
    ) / (left[0] * left_gap - right[0] * right_gap)
    margin = 0.05 * (fast - slow)
    contact = jnp.clip(contact, slow + margin, fast - margin)

    def conserved(fields, prim):
        return [prim[0], fields[1], fields[2], fields[3], fields[4]]

    def normal_flux(fields, prim, traction):
        speed = prim[1][direction]
        out = [fields[1 + direction]]
        for comp in range(3):
            out.append(fields[1 + comp] * speed + (traction if comp == direction else 0.0))
        out.append((fields[4] + traction) * speed)
        return out

    def star(fields, prim, wave, gap, traction):
        ratio = gap / (wave - contact)
        mass = prim[0] * ratio
        moment = [
            mass * contact if comp == direction else mass * prim[1][comp] for comp in range(3)
        ]
        energy = ratio * (
            fields[4] + (contact - prim[1][direction]) * (prim[0] * contact + traction / gap)
        )
        return [mass] + moment + [energy]

    flux_left = normal_flux(left_fields, left, left_traction)
    flux_right = normal_flux(right_fields, right, right_traction)
    state_left = conserved(left_fields, left)
    state_right = conserved(right_fields, right)
    star_left = star(left_fields, left, slow, left_gap, left_traction)
    star_right = star(right_fields, right, fast, right_gap, right_traction)
    result = []
    for comp in range(5):
        through_left = flux_left[comp] + slow * (star_left[comp] - state_left[comp])
        through_right = flux_right[comp] + fast * (star_right[comp] - state_right[comp])
        result.append(
            jnp.where(
                slow >= 0,
                flux_left[comp],
                jnp.where(
                    contact >= 0, through_left, jnp.where(fast > 0, through_right, flux_right[comp])
                ),
            )
        )
    for comp in range(3):
        if comp != direction:
            result[1 + comp] = result[1 + comp] - 0.5 * (
                left[3][comp][direction] + right[3][comp][direction]
            )
            result[4] = result[4] - 0.5 * (
                left[3][direction][comp] * left[1][comp]
                + right[3][direction][comp] * right[1][comp]
            )
    for row in range(3):
        flow_left = sum((left[2][row][comp] * left[1][comp] for comp in range(3)))
        flow_right = sum((right[2][row][comp] * right[1][comp] for comp in range(3)))
        jump = right_fields[5 + 3 * row + direction] - left_fields[5 + 3 * row + direction]
        blended = (fast * flow_left - slow * flow_right + slow * fast * jump) / (fast - slow)
        result.append(jnp.where(slow >= 0, flow_left, jnp.where(fast <= 0, flow_right, blended)))
    return result


def plastic(fields, label):
    gamma, stiff, shear, cohesion, friction = material(label)
    prim = primitives(fields, label)
    sandy = label == 0
    radius = jnp.where(sandy, cohesion + friction * jnp.maximum(prim[4], 0.0), 1.0)
    gradient = prim[2]
    for turn in range(RETURN_ITERS):
        stress, unused = deviator(gradient, shear)
        norm = jnp.sqrt(
            sum((stress[row][col] * stress[row][col] for row in range(3) for col in range(3)))
        )
        factor = jnp.where(sandy, 0.5 * (1.0 + radius / jnp.maximum(norm, radius)), 1.0)
        third = (gradient[0][0] + gradient[1][1] + gradient[2][2]) / 3.0
        gradient = [
            [
                factor * gradient[row][col] + ((1.0 - factor) * third if row == col else 0.0)
                for col in range(3)
            ]
            for row in range(3)
        ]
    return fields[:5] + [gradient[row][col] for row in range(3) for col in range(3)]


def sweep(padded, label_pad, axis, direction, step_size):
    cells = padded.shape[axis] - 6
    faces = cells + 1

    def part(array, offset, count):
        return lax.slice_in_dim(array, offset, offset + count, axis=axis)

    shifted = [part(padded, offset, faces) for offset in range(6)]
    left_state = weno_face(shifted[0], shifted[1], shifted[2], shifted[3], shifted[4])
    right_state = weno_face(shifted[5], shifted[4], shifted[3], shifted[2], shifted[1])
    left_label = part(label_pad, 2, faces)[0]
    right_label = part(label_pad, 3, faces)[0]
    fluxes = riemann(
        [left_state[comp] for comp in range(14)],
        [right_state[comp] for comp in range(14)],
        left_label,
        right_label,
        direction,
    )
    centre = part(padded, 3, cells)
    label = part(label_pad, 3, cells)[0]
    fields = [centre[comp] for comp in range(14)]
    changed = [0, 1, 2, 3, 4] + [5 + 3 * row + direction for row in range(3)]
    for slot in range(8):
        flux = fluxes[slot]
        change = lax.slice_in_dim(flux, 1, faces, axis=axis - 1) - lax.slice_in_dim(
            flux, 0, cells, axis=axis - 1
        )
        fields[changed[slot]] = fields[changed[slot]] - step_size * change
    return jnp.stack(plastic(fields, label))


def edge_pad(array, axis):
    widths = [(0, 0)] * array.ndim
    widths[axis] = (3, 3)
    return jnp.pad(array, widths, mode="edge")


def depth_via_owner(state, label_block, step_size):
    packed = jnp.concatenate([state, label_block], axis=0)
    columns = exchange_by_axis(packed, BA, (0, 1), 3, 1)
    swept = sweep(edge_pad(columns[:14], 1), edge_pad(columns[14:], 1), 1, 2, step_size)
    return exchange_by_axis(swept, BA, (0, 1), 1, 3)


def shards(state, labels):
    label_block = labels.astype(jnp.float32)[None]
    prim = primitives([state[comp] for comp in range(14)], label_block[0])
    fastest = jnp.maximum(
        jnp.maximum(jnp.abs(prim[1][0]), jnp.abs(prim[1][1])), jnp.abs(prim[1][2])
    )
    peak = over_axes(jnp.max(fastest + prim[5]), AA_BA)
    step_size = COURANT / peak
    state = sweep(edge_pad(state, 3), edge_pad(label_block, 3), 3, 0, step_size)
    packed = jnp.concatenate([state, label_block], axis=0)
    padded = padded_2(packed, ((AA, 2),), 3)
    position = lax.axis_index(AA)
    count = lax.axis_size(AA)
    lower = jnp.where(position == 0, jnp.repeat(padded[:, :, 3:4], 3, axis=2), padded[:, :, :3])
    upper = jnp.where(
        position == count - 1, jnp.repeat(padded[:, :, -4:-3], 3, axis=2), padded[:, :, -3:]
    )
    padded = jnp.concatenate([lower, padded[:, :, 3:-3], upper], axis=2)
    state = sweep(padded[:14], padded[14:], 2, 1, step_size)
    return depth_via_owner(state, label_block, step_size)


def solution(mesh):
    finer = Mesh(mesh.devices.reshape(4, 2, 2, 2, 32), ("aa_0", "aa_1", "aa_2", "ba_0", "ba_1"))
    placed = (P(None, BA, AA, None), P(BA, AA, None))
    return jax.shard_map(
        shards, mesh=finer, in_specs=placed, out_specs=P(None, BA, AA, None), check_vma=False
    )
```

profile of v0, /device:TPU:1, one launch (start us, length us, event | category | flops | bytes accessed | tf_op | source)
XLA Modules:
  0.0 197.0 jit_solution(10725312599483284405)
XLA Ops:
  0.0 0.8 fusion.392
  0.8 1.5 add_reduce_fusion
  2.3 10.2 %pmax.35 = f32[]{:T(128)} all-reduce(f32[]{:T(128)} %get-tuple-element.143), channel_id=1, replica_groups=mesh['aa_0'=4,'aa_1'=2,'aa_2'=2,'ba_0'=2,'ba_1'=32] {'aa_0'}, use_global_device_ids=true, to_apply=%region_1.2 | all-reduce | flops 1 | bytes 8 | tf_op jit(solution)/shard_map/pmax | solution.py:52
  12.7 5.9 %pmax.36 = f32[]{:T(128)} all-reduce(f32[]{:T(128)} %pmax.35), channel_id=1, replica_groups=mesh['aa_0'=4,'aa_1'=2,'aa_2'=2,'ba_0'=2,'ba_1'=32] {'aa_1'}, use_global_device_ids=true, to_apply=%region_2.3 | all-reduce | flops 1 | bytes 8 | tf_op jit(solution)/shard_map/pmax | solution.py:52
  19.1 0.7 add_divide_fusion.2
  20.2 16.2 %pmax.37 = f32[]{:T(128)} all-reduce(f32[]{:T(128)} %pmax.36), channel_id=1, replica_groups=mesh['aa_0'=4,'aa_1'=2,'aa_2'=2,'ba_0'=2,'ba_1'=32] {'aa_2'}, use_global_device_ids=true, to_apply=%region_3.4 | all-reduce | flops 1 | bytes 8 | tf_op jit(solution)/shard_map/pmax | solution.py:52
  36.4 4.4 %pmax.38 = f32[]{:T(128)} all-reduce(f32[]{:T(128)} %pmax.37), channel_id=1, replica_groups=mesh['aa_0'=4,'aa_1'=2,'aa_2'=2,'ba_0'=2,'ba_1'=32] {'ba_0'}, use_global_device_ids=true, to_apply=%region_4.5 | all-reduce | flops 1 | bytes 8 | tf_op jit(solution)/shard_map/pmax | solution.py:52
  40.9 46.5 %pmax.39 = f32[]{:T(128)} all-reduce(f32[]{:T(128)} %pmax.38), channel_id=1, replica_groups=mesh['aa_0'=4,'aa_1'=2,'aa_2'=2,'ba_0'=2,'ba_1'=32] {'ba_1'}, use_global_device_ids=true, to_apply=%region_5.6 | all-reduce | flops 1 | bytes 8 | tf_op jit(solution)/shard_map/pmax | solution.py:52
  88.5 17.4 %collective-permute-start.1 = (f32[15,1,3,128]{3,2,1,0:T(4,128)S(1)}, f32[15,1,3,128]{3,2,1,0:T(4,128)S(1)}, u32[]{:S(2)}, u32[]{:S(2)}) collective-permute-start(f32[15,1,3,128]{3,2,1,0:T(4,128)S(1)} %get-tuple-element.167), channel_id=1, source_target_pairs={{64,0},{128,64},{192,128},{256,192},{320,256},{384,320},{448,384},... | collective-permute-start | bytes 69128 | tf_op jit(solution)/shard_map/ppermute | solution.py:63
  105.9 4.6 %collective-permute-start = (f32[15,1,3,128]{3,2,1,0:T(4,128)S(1)}, f32[15,1,3,128]{3,2,1,0:T(4,128)S(1)}, u32[]{:S(2)}, u32[]{:S(2)}) collective-permute-start(f32[15,1,3,128]{3,2,1,0:T(4,128)S(1)} %get-tuple-element.168), channel_id=1, source_target_pairs={{0,64},{64,128},{128,192},{192,256},{256,320},{320,384},{384,448},... | collective-permute-start | bytes 69128 | tf_op jit(solution)/shard_map/ppermute | solution.py:60
  110.8 0.7 collective-permute-done
  111.5 0.3 add_divide_fusion.1
  115.6 5.1 %all_to_all.20 = f32[2,1,3840]{2,1,0:T(1,128)S(1)} all-to-all(f32[2,1,3840]{2,1,0:T(1,128)S(1)} %reshape.9952), channel_id=1, replica_groups=mesh['aa_0'=4,'aa_1'=2,'aa_2'=2,'ba_0'=2,'ba_1'=32] {'ba_0'}, dimensions={0} | all-to-all | bytes 61440 | tf_op jit(solution)/shard_map/all_to_all | solution.py:42
  120.7 0.5 broadcast.4290
  121.3 0.7 reduce.8
  122.1 0.2 copy.287
  122.4 0.3 reshape.9954
  122.7 36.0 %all_to_all.21 = f32[32,1,240]{2,1,0:T(1,128)S(1)} all-to-all(f32[32,1,240]{2,1,0:T(1,128)S(1)} %reshape.9954), channel_id=1, replica_groups=mesh['aa_0'=4,'aa_1'=2,'aa_2'=2,'ba_0'=2,'ba_1'=32] {'ba_1'}, dimensions={0} | all-to-all | bytes 61440 | tf_op jit(solution)/shard_map/all_to_all | solution.py:42
  158.6 0.7 reduce.9
  159.4 0.4 reshape.9955
  159.7 0.2 copy.303
  161.1 0.7 add_divide_fusion
  162.9 5.1 %all_to_all.22 = f32[2,1,3584]{2,1,0:T(1,128)S(1)} all-to-all(f32[2,1,3584]{2,1,0:T(1,128)S(1)} %reshape.9956), channel_id=1, replica_groups=mesh['aa_0'=4,'aa_1'=2,'aa_2'=2,'ba_0'=2,'ba_1'=32] {'ba_0'}, dimensions={0} | all-to-all | bytes 57344 | tf_op jit(solution)/shard_map/all_to_all | solution.py:42
  168.0 0.7 reduce.10
  168.9 0.3 copy.297
  169.2 0.4 reshape.9958
  169.6 24.9 %all_to_all.23 = f32[32,1,224]{2,1,0:T(1,128)S(1)} all-to-all(f32[32,1,224]{2,1,0:T(1,128)S(1)} %reshape.9958), channel_id=1, replica_groups=mesh['aa_0'=4,'aa_1'=2,'aa_2'=2,'ba_0'=2,'ba_1'=32] {'ba_1'}, dimensions={0} | all-to-all | bytes 57344 | tf_op jit(solution)/shard_map/all_to_all | solution.py:42
  194.5 0.7 reduce.11
  195.3 0.4 reshape.9959
  195.7 0.2 copy.298
  196.0 0.2 copy.299
  196.2 0.7 copy.300
  (144 shorter events, 7.9 us)
Async XLA Ops:
  0.0 0.8 copy-start.1
  0.0 2.2 %copy-start = (f32[14,1,4,128]{3,2,1,0:T(4,128)S(1)}, f32[14,1,4,128]{3,2,1,0:T(4,128)}, u32[]{:S(2)}) copy-start(f32[14,1,4,128]{3,2,1,0:T(4,128)} %param.2) | copy-start | bytes 86020
  88.5 22.2 %collective-permute-start.1 = (f32[15,1,3,128]{3,2,1,0:T(4,128)S(1)}, f32[15,1,3,128]{3,2,1,0:T(4,128)S(1)}, u32[]{:S(2)}, u32[]{:S(2)}) collective-permute-start(f32[15,1,3,128]{3,2,1,0:T(4,128)S(1)} %get-tuple-element.167), channel_id=1, source_target_pairs={{64,0},{128,64},{192,128},{256,192},{320,256},{384,320},{448,384},... | collective-permute-start | bytes 69128 | tf_op jit(solution)/shard_map/ppermute | solution.py:63
  105.9 5.5 %collective-permute-start = (f32[15,1,3,128]{3,2,1,0:T(4,128)S(1)}, f32[15,1,3,128]{3,2,1,0:T(4,128)S(1)}, u32[]{:S(2)}, u32[]{:S(2)}) collective-permute-start(f32[15,1,3,128]{3,2,1,0:T(4,128)S(1)} %get-tuple-element.168), channel_id=1, source_target_pairs={{0,64},{64,128},{128,192},{192,256},{256,320},{320,384},{384,448},... | collective-permute-start | bytes 69128 | tf_op jit(solution)/shard_map/ppermute | solution.py:60
where the time goes:
time: 201 us; the launch traced here: 197 us
  blocking collectives  154 us (77%)
  starting transfers between devices  22 us (11%)
  local copies, waits for them, and re-layouts  10.2 us (5%)
  other arithmetic  8.3 us (4%)
    pmax x5, blocking collectives, over_axes(): return functools.reduce(lax.pmax, axes, value)  83.3 us
    all_to_all x4, blocking collectives, exchange_in_order(): lax.all_to_all(pieces, axes[k], split_axis=k, concat_axis=k, tiled=True)  71.2 us
    ppermute x1, starting transfers between devices, padded_2(): lax.ppermute(lax.slice_in_dim(block, 0, width, axis=dim), axis, backward)  17.4 us
    ppermute x1, starting transfers between devices, padded_2(): lax.ppermute(lax.slice_in_dim(block, block.shape[dim] - width, None, axis...  4.56 us
  transfers between devices with their start and end apart: 2, of which 1 were waited for; matrix products, arithmetic and copies ran while one was open for 0% of the time, Pallas kernels for 0%

commit v1 on v0

v1 whole, which is shorter than its diff:
```python
import jax
import jax.numpy as jnp
from jax import lax
from jax.experimental import pallas as pl
from jax.experimental.pallas import tpu as pltpu
from jax.sharding import PartitionSpec as P

MESH = pl.DeviceIdType.MESH
COURANT = 0.4
EPS = 1e-06
NA, NB, NZC = 16, 64, 32
REACH = 8
ROWS = 80
F32 = jnp.float32


def pick(label, sand, solid, void):
    return jnp.where(label == 0.0, sand, jnp.where(label == 1.0, solid, void))


def deviator(g):
    def dot(i, j):
        return g[i] * g[j] + g[3 + i] * g[3 + j] + g[6 + i] * g[6 + j]

    xx, yy, zz = dot(0, 0), dot(1, 1), dot(2, 2)
    third = (xx + yy + zz) * (1.0 / 3.0)
    return (xx - third, yy - third, zz - third, dot(0, 1), dot(0, 2), dot(1, 2))


def squares(dev):
    return (
        dev[0] * dev[0]
        + dev[1] * dev[1]
        + dev[2] * dev[2]
        + 2.0 * (dev[3] * dev[3] + dev[4] * dev[4] + dev[5] * dev[5])
    )


def primitives(fields, label):
    gamma = pick(label, 3.0, 4.0, 1.4)
    stiff = pick(label, 1.0, 6.0, 0.0)
    shear = pick(label, 0.6, 3.0, 0.0)
    density = jnp.maximum(fields[0], 0.2)
    inverse = 1.0 / density
    velocity = [fields[1 + k] * inverse for k in range(3)]
    dev = deviator(fields[5:14])
    energy = 0.25 * shear * squares(dev)
    kinetic = 0.5 * (
        fields[1] * velocity[0] + fields[2] * velocity[1] + fields[3] * velocity[2]
    )
    pressure = (gamma - 1.0) * (fields[4] - kinetic - energy) - gamma * stiff
    sound = jnp.sqrt(
        (gamma * jnp.maximum(pressure + stiff, 0.1) + (4.0 / 3.0) * shear) * inverse
    )
    return density, velocity, dev, shear, pressure, sound


OFF = {(0, 1): 3, (1, 0): 3, (0, 2): 4, (2, 0): 4, (1, 2): 5, (2, 1): 5}


def riemann(left, right, label_left, label_right, d):
    rl, ul, dl, ml, pl_, cl = primitives(left, label_left)
    rr, ur, dr, mr, pr, cr = primitives(right, label_right)
    slow = jnp.minimum(ul[d] - cl, ur[d] - cr)
    fast = jnp.maximum(ul[d] + cl, ur[d] + cr)
    tl = pl_ + ml * dl[d]
    tr = pr + mr * dr[d]
    gl = slow - ul[d]
    gr = fast - ur[d]
    al = rl * gl
    ar = rr * gr
    contact = (tr - tl + al * ul[d] - ar * ur[d]) / (al - ar)
    margin = 0.05 * (fast - slow)
    contact = jnp.minimum(jnp.maximum(contact, slow + margin), fast - margin)
    is_left = contact >= 0.0

    def side(x, y):
        return jnp.where(is_left, x, y)

    r = side(rl, rr)
    m = [side(left[1 + k], right[1 + k]) for k in range(3)]
    e = side(left[4], right[4])
    u = side(ul[d], ur[d])
    t = side(tl, tr)
    wave = side(slow, fast)
    gap = side(gl, gr)
    active = jnp.where(is_left, -slow, fast) > 0.0
    over = 1.0 / (wave - contact)
    chi = gap * over
    mass = r * chi
    energy = chi * (e + (contact - u) * (r * contact)) + (contact - u) * t * over
    jump = [mass - r]
    for k in range(3):
        jump.append(mass * contact - m[k] if k == d else chi * m[k] - m[k])
    jump.append(energy - e)
    flux = [m[d]]
    for k in range(3):
        flux.append(m[k] * u + t if k == d else m[k] * u)
    flux.append((e + t) * u)
    out = [flux[k] + jnp.where(active, wave * jump[k], 0.0) for k in range(5)]
    hl, hr = 0.5 * ml, 0.5 * mr
    for k in range(3):
        if k != d:
            o = OFF[(k, d)]
            sl, sr = hl * dl[o], hr * dr[o]
            out[1 + k] = out[1 + k] + (sl + sr)
            out[4] = out[4] + (sl * ul[k] + sr * ur[k])
    span = 1.0 / (fast - slow)
    both = slow * fast
    for i in range(3):
        b = 5 + 3 * i
        fl = left[b] * ul[0] + left[b + 1] * ul[1] + left[b + 2] * ul[2]
        fr = right[b] * ur[0] + right[b + 1] * ur[1] + right[b + 2] * ur[2]
        mix = (fast * fl - slow * fr + both * (right[b + d] - left[b + d])) * span
        out.append(jnp.where(slow >= 0.0, fl, jnp.where(fast <= 0.0, fr, mix)))
    return out


def plastic(fields, label):
    sandy = label == 0.0
    g = fields[5:14]
    dev = deviator(g)
    sq = squares(dev)
    kinetic = (
        0.5
        * (fields[1] * fields[1] + fields[2] * fields[2] + fields[3] * fields[3])
        / jnp.maximum(fields[0], 0.2)
    )
    pressure = 2.0 * (fields[4] - kinetic - 0.15 * sq) - 3.0
    radius = 0.05 + 0.4 * jnp.maximum(pressure, 0.0)
    cur = g
    for turn in range(2):
        if turn:
            sq = squares(deviator(cur))
        norm = 0.6 * jnp.sqrt(sq)
        factor = 0.5 * (1.0 + radius / jnp.maximum(norm, radius))
        shift = (1.0 - factor) * ((cur[0] + cur[4] + cur[8]) * (1.0 / 3.0))
        cur = [factor * cur[k] + shift if k % 4 == 0 else factor * cur[k] for k in range(9)]
    return list(fields[:5]) + [jnp.where(sandy, cur[k], g[k]) for k in range(9)]


def smooth(d1, d2, d3, d4):
    s1, s2, s3 = d2 - d1, d3 - d2, d4 - d3
    w1, w2, w3 = 3.0 * d2 - d1, d2 + d3, d4 - 3.0 * d3
    c = 13.0 / 12.0
    qa = 1.0 / (EPS + c * (s1 * s1) + 0.25 * (w1 * w1))
    qb = 1.0 / (EPS + c * (s2 * s2) + 0.25 * (w2 * w2))
    qc = 1.0 / (EPS + c * (s3 * s3) + 0.25 * (w3 * w3))
    return qa * qa, 6.0 * (qb * qb), qc * qc


def weno_plus(q, d1, d2, d3, d4):
    qa, qb, qc = q
    qc = 3.0 * qc
    top = qa * (5.0 * d2 - 2.0 * d1) + qb * (d2 + 2.0 * d3) + qc * (4.0 * d3 - d4)
    return top / (6.0 * (qa + qb + qc))


def weno_minus(q, d1, d2, d3, d4):
    qa, qb, qc = q
    qa = 3.0 * qa
    top = qc * (2.0 * d4 - 5.0 * d3) - qb * (d3 + 2.0 * d2) + qa * (d1 - 4.0 * d2)
    return top / (6.0 * (qa + qb + qc))


def end_delta(d):
    t = 1.0 / (1.0 + (4.0 / 3.0 / EPS) * (d * d))
    t = t * t
    return d * (0.05 * t) / (0.7 + 0.3 * t)


def lane_iota(shape):
    return lax.broadcasted_iota(jnp.int32, shape, len(shape) - 1)


def changed(d):
    return [0, 1, 2, 3, 4] + [5 + 3 * i + d for i in range(3)]


def row(r):
    if isinstance(r, int):
        return pl.ds(r * 8, 8)
    return pl.ds(pl.multiple_of(r * 8, 8), 8)


def x_faces(source, r, flux_ref, ends_left, ends_right, slot):
    lane = lane_iota((8, 128))
    first, last = lane == 0, lane == 127
    here = lane == slot
    left, right = [], []
    for f in range(14):
        s = source(f)
        up = jnp.where(last, 0.0, pltpu.roll(s, 127, 1) - s)
        d3 = up
        d2 = pltpu.roll(up, 1, 1)
        d1 = jnp.where(first, 0.0, pltpu.roll(up, 2, 1))
        d4 = jnp.where(last, 0.0, pltpu.roll(up, 127, 1))
        q = smooth(d1, d2, d3, d4)
        plus = s + weno_plus(q, d1, d2, d3, d4)
        minus = s + weno_minus(q, d1, d2, d3, d4)
        g = end_delta(jnp.where(last, d2, up))
        left.append(jnp.where(first, s - g, pltpu.roll(plus, 1, 1)))
        right.append(minus)
        ends_left[f] = jnp.where(here, plus[:, 127:128], ends_left[f])
        ends_right[f] = jnp.where(here, (s + g)[:, 127:128], ends_right[f])
    label = source(14)
    ends_left[14] = jnp.where(here, label[:, 127:128], ends_left[14])
    label_left = jnp.where(first, label, pltpu.roll(label, 1, 1))
    fluxes = riemann(left, right, label_left, label, 0)
    for k in range(8):
        flux_ref[k, row(slot)] = fluxes[k]


def x_ends(ends_left, ends_right, end_flux):
    left = [ends_left[f] for f in range(14)]
    right = [ends_right[f] for f in range(14)]
    label = ends_left[14]
    fluxes = riemann(left, right, label, label, 0)
    for k in range(8):
        end_flux[k] = fluxes[k]


def x_update(source, r, flux_ref, end_flux, step, after):
    lane = lane_iota((8, 128))
    last = lane == 127
    fields = [source(f) for f in range(14)]
    for k, f in enumerate(changed(0)):
        flux = flux_ref[k, row(r)]
        end = jnp.sum(jnp.where(lane == r, end_flux[k], 0.0), axis=1, keepdims=True)
        upper = jnp.where(last, end, pltpu.roll(flux, 127, 1))
        fields[f] = fields[f] - step * (upper - flux)
    fields = plastic(fields, source(14))
    for f in range(14):
        after[f, row(r)] = fields[f]


def y_states(after, c, plus_ref, minus_ref):
    for f in range(14):
        s = [after[f, row(c + k)] for k in range(-2, 3)]
        d1, d2, d3, d4 = [s[k + 1] - s[k] for k in range(4)]
        q = smooth(d1, d2, d3, d4)
        plus_ref[f, row(c - 2)] = s[2] + weno_plus(q, d1, d2, d3, d4)
        minus_ref[f, row(c - 2)] = s[2] + weno_minus(q, d1, d2, d3, d4)


def y_flux(j, plus_ref, minus_ref, label_of, flux_ref):
    left = [plus_ref[f, row(j)] for f in range(14)]
    right = [minus_ref[f, row(j + 1)] for f in range(14)]
    fluxes = riemann(left, right, label_of(j + 2), label_of(j + 3), 1)
    for k in range(8):
        flux_ref[k, row(j)] = fluxes[k]


def y_update(j, after, label_of, flux_ref, step, done):
    fields = [after[f, row(j + 3)] for f in range(14)]
    for k, f in enumerate(changed(1)):
        fields[f] = fields[f] - step * (flux_ref[k, row(j + 1)] - flux_ref[k, row(j)])
    fields = plastic(fields, label_of(j + 3))
    for f in range(14):
        start = (f * 4 + j) * 8
        done[pl.ds(start, 8)] = fields[f]


def z_sweep(done, layer_label, step, out):
    low = lax.broadcasted_iota(jnp.int32, (8, 128), 0) < 4

    def swap(x):
        return pltpu.roll(x, 4, 0)

    left, right, centre = [], [], []
    for p in range(7):
        s = [done[pl.ds(p * 64 + o, 8, stride=8)] for o in range(7)]
        d = [s[k + 1] - s[k] for k in range(6)]
        q2 = smooth(*d[0:4])
        q3 = smooth(*d[1:5])
        q4 = smooth(*d[2:6])
        l_low = s[2] + weno_plus(q2, *d[0:4])
        r_low = s[3] + weno_minus(q3, *d[1:5])
        l_up = s[3] + weno_plus(q3, *d[1:5])
        r_up = s[4] + weno_minus(q4, *d[2:6])
        left += [jnp.where(low, l_low, swap(l_up)), jnp.where(low, swap(l_low), l_up)]
        right += [jnp.where(low, r_low, swap(r_up)), jnp.where(low, swap(r_low), r_up)]
        centre += [s[3], swap(s[3])]
    lab2, lab3, lab4 = layer_label(2), layer_label(3), layer_label(4)
    fluxes = riemann(
        left, right, jnp.where(low, lab2, swap(lab3)), jnp.where(low, lab3, swap(lab4)), 2
    )
    for k, f in enumerate(changed(2)):
        centre[f] = centre[f] - step * (swap(fluxes[k]) - fluxes[k])
    fields = plastic(centre, lab3)
    for f in range(14):
        out[f, 0] = fields[f][0:4]


def clamped(r, place):
    low = jnp.where(place == 0, 3, 0)
    high = jnp.where(place == NA - 1, 6, 9)
    return jnp.minimum(jnp.maximum(r, low), high)


def compute_body(place, halo, peak, out, flux_x, ends_left, ends_right, end_flux, after,
                 plus_ref, minus_ref, flux_y, done):
    step = COURANT / jnp.max(peak[...], keepdims=True)

    def source_of(r):
        at = row(clamped(r, place))
        return lambda f: halo[f, at]

    ends_left[...] = jnp.ones_like(ends_left)
    ends_right[...] = jnp.ones_like(ends_right)

    def faces(r, carry):
        x_faces(source_of(r), r, flux_x, ends_left, ends_right, r)
        return carry

    lax.fori_loop(0, 10, faces, 0)
    x_ends(ends_left, ends_right, end_flux)

    def update(r, carry):
        x_update(source_of(r), r, flux_x, end_flux, step, after)
        return carry

    lax.fori_loop(0, 10, update, 0)

    def states(i, carry):
        y_states(after, i + 2, plus_ref, minus_ref)
        return carry

    lax.fori_loop(0, 6, states, 0)

    def label_of(r):
        return source_of(r)(14)

    for j in range(5):
        y_flux(j, plus_ref, minus_ref, label_of, flux_y)
    for j in range(4):
        y_update(j, after, label_of, flux_y, step, done)

    def layer_label(o):
        return pltpu.roll(halo[14, pl.ds(o, 8, stride=8)], 5, 0)

    z_sweep(done, layer_label, step, out)


COMPUTE_SCRATCH = [
    pltpu.VMEM((8, ROWS, 128), F32),
    pltpu.VMEM((15, 8, 128), F32),
    pltpu.VMEM((14, 8, 128), F32),
    pltpu.VMEM((8, 8, 128), F32),
    pltpu.VMEM((14, ROWS, 128), F32),
    pltpu.VMEM((14, 48, 128), F32),
    pltpu.VMEM((14, 48, 128), F32),
    pltpu.VMEM((8, 40, 128), F32),
    pltpu.VMEM((448, 128), F32),
]


def compute_kernel(*refs):
    compute_body(lax.axis_index("aa"), *refs)


def gather_kernel(state, labels, halo, peak, layers, marks, m0, r1, m1, ra, m2, rb,
                  local_sem, z_send, z_recv, l_send, l_recv, y_send, y_recv, m_send, m_recv):
    a, b = lax.axis_index("aa"), lax.axis_index("ba")
    xl, z = b // NZC, b % NZC
    barrier = pltpu.get_barrier_semaphore()

    def plane(t):
        i = (a * 2 + xl + t) % (2 * NA)
        return (i // 2, (i % 2) * NZC + z)

    def ring(k):
        return (a, xl * NZC + (z + (k + NZC)) % NZC)

    def along(k):
        return (a, (b + (k + NB)) % NB)

    def across(k):
        return ((a + (k + NA)) % NA, b)

    def greet(device):
        pl.semaphore_signal(barrier, inc=1, device_id=device, device_id_type=MESH)

    near = (1, -1, 2, -2, 3, -3)
    for k in near:
        greet(along(k))

    def greet_plane(t, carry):
        greet(plane(t))
        return carry

    def greet_ring(k, carry):
        greet(ring(k))
        greet(ring(-k))
        return carry

    lax.fori_loop(1, REACH + 1, greet_ring, 0)
    lax.fori_loop(1, 2 * NA, greet_plane, 0)
    own_state = pltpu.make_async_copy(state.at[:, 0], layers.at[3], local_sem.at[0])
    own_label = pltpu.make_async_copy(labels.at[0], marks.at[3], local_sem.at[1])
    own_state.start()
    own_label.start()
    own_state.wait()
    own_label.wait()
    fields = [layers[3, f] for f in range(14)]
    label = marks[3].astype(F32)
    density, velocity, dev, shear, pressure, sound = primitives(fields, label)
    speed = sound + jnp.maximum(
        jnp.maximum(jnp.abs(velocity[0]), jnp.abs(velocity[1])), jnp.abs(velocity[2])
    )
    m0[...] = jnp.max(speed, axis=0, keepdims=True)
    pl.semaphore_wait(barrier, len(near) + 2 * REACH + 2 * NA - 1)

    def copy(src, dst, send, recv, device):
        return pltpu.make_async_remote_copy(
            src_ref=src, dst_ref=dst, send_sem=send, recv_sem=recv,
            device_id=device, device_id_type=MESH,
        )

    def send_plane(t, carry):
        copy(m0, r1.at[t - 1], m_send.at[0], m_recv.at[0], plane(t)).start()
        return carry

    lax.fori_loop(1, 2 * NA, send_plane, 0)
    z_copies = []
    for i, k in enumerate(near):
        z_copies.append(
            copy(layers.at[3], layers.at[3 - k], z_send.at[i], z_recv.at[i], along(k))
        )
        z_copies.append(
            copy(marks.at[3], marks.at[3 - k], l_send.at[i], l_recv.at[i], along(k))
        )
    for c in z_copies:
        c.start()
    all_plane = copy(r1, r1, m_send.at[0], m_recv.at[0], plane(1))
    all_plane.wait_recv()
    m1[...] = jnp.maximum(m0[...], jnp.max(r1[...], axis=0))

    def send_ring(k, carry):
        copy(m1, ra.at[k - 1], m_send.at[1], m_recv.at[1], ring(k)).start()
        copy(m1, ra.at[REACH + k - 1], m_send.at[1], m_recv.at[1], ring(-k)).start()
        return carry

    lax.fori_loop(1, REACH + 1, send_ring, 0)
    for c in z_copies:
        c.wait_recv()
    for slot in range(7):
        at = jnp.minimum(jnp.maximum(b + (slot - 3), 0), NB - 1) - b + 3
        for f in range(14):
            halo[f, pl.ds(24 + slot, 4, stride=8)] = layers[at, f]
        halo[14, pl.ds(24 + slot, 4, stride=8)] = marks[at].astype(F32)
    for f in range(15):
        halo[f, pl.ds(24 + 7, 4, stride=8)] = halo[f, pl.ds(24 + 6, 4, stride=8)]
    y_copies = [
        copy(halo.at[:, pl.ds(32, 24)], halo.at[:, pl.ds(0, 24)], y_send.at[0], y_recv.at[0], across(1)),
        copy(halo.at[:, pl.ds(24, 24)], halo.at[:, pl.ds(56, 24)], y_send.at[1], y_recv.at[1], across(-1)),
    ]
    for c in y_copies:
        c.start()
    all_ring = copy(ra, ra, m_send.at[1], m_recv.at[1], ring(1))
    all_ring.wait_recv()
    m2[...] = jnp.maximum(m1[...], jnp.max(ra[...], axis=0))
    far = [
        copy(m2, rb.at[0], m_send.at[2], m_recv.at[2], ring(REACH)),
        copy(m2, rb.at[1], m_send.at[3], m_recv.at[3], ring(-REACH)),
    ]
    for c in far:
        c.start()
    for c in y_copies:
        c.wait_recv()
    for c in far:
        c.wait_recv()
    total = jnp.maximum(m2[...], jnp.maximum(rb[0], rb[1]))
    peak[...] = jnp.broadcast_to(total, (8, 128))
    all_plane.wait_send()
    all_ring.wait_send()
    for c in z_copies + y_copies + far:
        c.wait_send()


GATHER_SCRATCH = [
    pltpu.VMEM((7, 14, 4, 128), F32),
    pltpu.VMEM((7, 4, 128), jnp.int32),
    pltpu.VMEM((1, 128), F32),
    pltpu.VMEM((2 * NA - 1, 1, 128), F32),
    pltpu.VMEM((1, 128), F32),
    pltpu.VMEM((2 * REACH, 1, 128), F32),
    pltpu.VMEM((1, 128), F32),
    pltpu.VMEM((2, 1, 128), F32),
    pltpu.SemaphoreType.DMA((2,)),
    pltpu.SemaphoreType.DMA((6,)),
    pltpu.SemaphoreType.DMA((6,)),
    pltpu.SemaphoreType.DMA((6,)),
    pltpu.SemaphoreType.DMA((6,)),
    pltpu.SemaphoreType.DMA((2,)),
    pltpu.SemaphoreType.DMA((2,)),
    pltpu.SemaphoreType.DMA((4,)),
    pltpu.SemaphoreType.DMA((4,)),
]

VM = pl.BlockSpec(memory_space=pltpu.VMEM)


def shards(state, labels):
    halo, peak = pl.pallas_call(
        gather_kernel,
        out_shape=[
            jax.ShapeDtypeStruct((15, ROWS, 128), F32),
            jax.ShapeDtypeStruct((8, 128), F32),
        ],
        in_specs=[pl.BlockSpec(memory_space=pl.ANY)] * 2,
        out_specs=[VM, VM],
        scratch_shapes=GATHER_SCRATCH,
        compiler_params=pltpu.CompilerParams(collective_id=0, has_side_effects=True),
        name="gather",
    )(state, labels)
    return pl.pallas_call(
        compute_kernel,
        out_shape=jax.ShapeDtypeStruct((14, 1, 4, 128), F32),
        in_specs=[VM, VM],
        out_specs=VM,
        scratch_shapes=COMPUTE_SCRATCH,
        name="compute",
    )(halo, peak)


def solution(mesh):
    return jax.shard_map(
        shards,
        mesh=mesh,
        in_specs=(P(None, "ba", "aa", None), P("ba", "aa", None)),
        out_specs=P(None, "ba", "aa", None),
        check_vma=False,
    )
```

time: 201 us -> 53.4 us (0.27); the launches traced: 197 us -> 53.2 us
  blocking collectives: 154 us -> 0 us
  Pallas kernels: 0 us -> 53.2 us
  starting transfers between devices: 22 us -> 0 us
  local copies, waits for them, and re-layouts: 10.2 us -> 0 us
  other arithmetic: 8.3 us -> 0 us
    pmax x5 -> x0, blocking collectives: 83.3 us -> none  [over_axes(): return functools.reduce(lax.pmax, axes, value)]
    all_to_all x4 -> x0, blocking collectives: 71.2 us -> none  [exchange_in_order(): lax.all_to_all(pieces, axes[k], split_axis=k, concat_axis=k, tiled=True)]
    pallas_call x0 -> x2, Pallas kernels: none -> 53.2 us  [the longest x1 43.6 us: shards(): pl.pallas_call(gather_kernel, out_shape=[jax.ShapeDtypeStruct((15, ROWS,...]
    ppermute x2 -> x0, starting transfers between devices: 22 us -> none  [the longest x1 17.4 us: padded_2(): lax.ppermute(lax.slice_in_dim(block, 0, width, axis=dim), axis, backward)]
    all_to_all x4 -> x0, other arithmetic: 2.9 us -> none  [exchange_in_order(): lax.all_to_all(pieces, axes[k], split_axis=k, concat_axis=k, tiled=True)]
    unnamed x43 -> x0, local copies, waits for them, and re-layouts: 2.23 us -> none
    reshape x16 -> x0, local copies, waits for them, and re-layouts: 2.19 us -> none  [the longest x1 0.73 us: joined_along(): return jnp.moveaxis(pieces, 0, dim).reshape(lengths)]
  transfers between devices with their start and end apart: 2 -> 0, of which waited for: 1 -> 0; matrix products, arithmetic and copies ran while one was open for 0% -> 0% of each run, Pallas kernels for 0% -> 0%
where the time goes in v1:
time: 53.4 us; the launch traced here: 53.2 us
  Pallas kernels  53.2 us (100%)
    pallas_call x1, Pallas kernels, shards(): pl.pallas_call(gather_kernel, out_shape=[jax.ShapeDtypeStruct((15, ROWS,...  43.6 us
    pallas_call x1, Pallas kernels, shards(): pl.pallas_call(compute_kernel, out_shape=jax.ShapeDtypeStruct((14, 1, 4,...  9.52 us

profile of v1, /device:TPU:1, one launch (start us, length us, event | category | flops | bytes accessed | tf_op | source)
XLA Modules:
  0.0 53.2 jit_solution(12160081745412480725)
XLA Ops:
  0.0 43.6 %gather.1 = (f32[15,80,128]{2,1,0:T(8,128)}, f32[8,128]{1,0:T(8,128)}) custom-call(f32[14,1,4,128]{3,2,1,0:T(4,128)} %state.1, s32[1,4,128]{2,1,0:T(4,128)} %labels.1), custom_call_target="tpu_custom_call" | custom-call | tf_op jit(solution)/shard_map/gather/pallas_call | solution.py:505
  43.6 9.5 %compute.1 = f32[14,1,4,128]{3,2,1,0:T(4,128)} custom-call(f32[15,80,128]{2,1,0:T(8,128)} %get-tuple-element.7.refs_0_, f32[8,128]{1,0:T(8,128)} %get-tuple-element.8.refs_1_), custom_call_target="tpu_custom_call" | custom-call | tf_op jit(solution)/shard_map/compute/pallas_call | solution.py:517
